TPU v7x, 32 devices: a whole 2x2x4 slice. The times are simulated.
32 devices in a mesh: dp: 4 (over z), expert: 8 (over y, x, core).
Axes of the slice: x: 2, y: 2, z: 4, core: 2. Of those that a mesh axis runs over, the one named last changes fastest.
Arguments:
- tokens: bfloat16 [256, 192, 1024], P(None, ('dp', 'expert')), may hold values from -200 to 200
- grad_out: bfloat16 [256, 192, 1024], P(None, ('dp', 'expert')), may hold values from -6 to 6
- slot_out: bfloat16 [512, 192, 1024], P('expert', 'dp'), may hold values from -6 to 6
- slot_params: bfloat16 [512, 1024], P('expert'), may hold values from -2 to 2
Outputs:
- grad_tokens: bfloat16 [256, 192, 1024], P(None, ('dp', 'expert'))
- grad_slot_out: bfloat16 [512, 192, 1024], P('expert', 'dp')
- grad_params: float32 [512, 1024], P('expert', 'dp')
All inputs are finite; a program needn't handle non-finite values.
Results may differ from a plain program's by a relative error of at most 0.018.
Values may be sent and summed in bfloat16 or wider, within the bound.
No kernel may reach another device: no remote copies, remote signals or barrier semaphores. Data moves between devices by JAX's collectives and lax.ppermute only.
A program may use at most 128 MiB of HBM per device.

v0:
```python
import jax
import jax.numpy as jnp
from jax import lax
from jax.experimental import pallas as pl
from jax.experimental.pallas import tpu as pltpu
from jax.sharding import PartitionSpec as P


UNITS = 4
OUT_UNITS = (1, 3)
BACK_UNITS = (3, 1)
LANES = 256


def partners(size, step):
    return [(i, i ^ step) for i in range(size)]


def trade(x, axis, step):
    return lax.ppermute(x, axis, partners(lax.axis_size(axis), step))


def gather_params(slot_params, owners, shards):
    shard = lax.axis_index("dp")
    _, width = slot_params.shape
    cols = width // shards
    mine = lax.dynamic_slice_in_dim(slot_params, shard * cols, cols, axis=1)
    blocks = [mine]
    for k in range(1, owners):
        blocks.append(trade(mine, "expert", k))
    part = jnp.concatenate(lax.optimization_barrier(blocks), axis=0)
    parts = [part]
    for j in range(1, shards):
        parts.append(trade(part, "dp", j))
    parts = jnp.stack(lax.optimization_barrier(parts))
    return jnp.concatenate(
        [lax.dynamic_index_in_dim(parts, j ^ shard, 0, keepdims=False) for j in range(shards)],
        axis=1,
    )


def split_kernel(me_ref, x_ref, *refs):
    outs, stage = refs[:-1], refs[-1]
    turned = x_ref[...].astype(jnp.float32).transpose(1, 0, 2).astype(x_ref.dtype)
    stage[...] = turned.reshape(stage.shape)
    for k, out in enumerate(outs):
        out[...] = stage[me_ref[0] ^ k]


def split_slots(slot_out, me, owners, first, units):
    own_slots, img_all, width = slot_out.shape
    unit, images = own_slots // UNITS, img_all // owners
    block = pl.BlockSpec((images, unit, LANES), lambda u, j, me: (0, u, j))
    return pl.pallas_call(
        split_kernel,
        out_shape=[jax.ShapeDtypeStruct((images, units * unit, width), slot_out.dtype)] * owners,
        grid_spec=pltpu.PrefetchScalarGridSpec(
            num_scalar_prefetch=1,
            grid=(units, width // LANES),
            in_specs=[pl.BlockSpec((unit, img_all, LANES), lambda u, j, me: (first + u, 0, j))],
            out_specs=[block] * owners,
            scratch_shapes=[pltpu.VMEM((owners, images, unit, LANES), slot_out.dtype)],
        ),
    )(me[None], slot_out)


def join_kernel(me_ref, *refs):
    stage, out = refs[-1], refs[-2]
    owners, images, unit, lanes = stage.shape
    for k in range(owners):
        stage[me_ref[0] ^ k] = refs[k][...]
    rows = stage[...].reshape(owners * images, unit, lanes)
    out[...] = rows.astype(jnp.float32).transpose(1, 0, 2).astype(out.dtype)


def join_slots(blocks, whole, me, own_slots, first, units):
    owners = len(blocks)
    images, _, width = blocks[0].shape
    unit = own_slots // UNITS
    block = pl.BlockSpec((images, unit, LANES), lambda u, j, me: (0, u, j))
    in_specs, extra, aliases = [block] * owners, [], {}
    if whole is not None:
        in_specs, extra, aliases = in_specs + [pl.BlockSpec(memory_space=pl.ANY)], [whole], {owners + 1: 0}
    return pl.pallas_call(
        join_kernel,
        out_shape=jax.ShapeDtypeStruct((own_slots, owners * images, width), blocks[0].dtype),
        grid_spec=pltpu.PrefetchScalarGridSpec(
            num_scalar_prefetch=1,
            grid=(units, width // LANES),
            in_specs=in_specs,
            out_specs=pl.BlockSpec(
                (unit, owners * images, LANES), lambda u, j, me: (first + u, 0, j)
            ),
            scratch_shapes=[pltpu.VMEM((owners, images, unit, LANES), blocks[0].dtype)],
        ),
        input_output_aliases=aliases,
    )(me[None], *blocks, *extra)


def fetch_outputs(slot_out, owners, me):
    parts, first = [], 0
    for units in OUT_UNITS:
        blocks = split_slots(slot_out, me, owners, first, units)
        got = [blocks[0]]
        for k in range(1, owners):
            got.append(trade(blocks[k], "expert", k))
        parts.append(got)
        first += units
    parts = lax.optimization_barrier(parts)
    return jnp.concatenate([part[k] for k in range(owners) for part in parts], axis=1)


def return_grads(grad_slot, owners, me):
    _, all_slots, _ = grad_slot.shape
    own_slots = all_slots // owners
    unit = own_slots // UNITS
    out, first = None, 0
    for units in BACK_UNITS:
        blocks = []
        for k in range(owners):
            at = k * own_slots + first * unit
            block = grad_slot[:, at : at + units * unit]
            blocks.append(trade(block, "expert", k) if k else block)
        out = join_slots(blocks, out, me, own_slots, first, units)
        first += units
    return out


def reduce_params(param_part, owners, shards):
    shard = lax.axis_index("dp")
    all_slots, width = param_part.shape
    cols, own_slots = width // shards, all_slots // owners
    low = param_part.astype(jnp.bfloat16)
    total = lax.dynamic_slice_in_dim(param_part, shard * cols, cols, axis=1)
    for j in range(1, shards):
        block = lax.dynamic_slice_in_dim(low, (shard ^ j) * cols, cols, axis=1)
        total = total + trade(block, "dp", j).astype(jnp.float32)
    low = total.astype(jnp.bfloat16)
    owned = total[:own_slots]
    for k in range(1, owners):
        block = low[k * own_slots : (k + 1) * own_slots]
        owned = owned + trade(block, "expert", k).astype(jnp.float32)
    return owned


def per_device(tokens, grad_out, slot_out, slot_params):
    owners, shards = lax.axis_size("expert"), lax.axis_size("dp")
    me = lax.axis_index("expert")
    all_params = gather_params(slot_params, owners, shards)
    slot_rows = fetch_outputs(slot_out, owners, me)
    logits = jnp.einsum("tbd,sd->tbs", tokens, all_params, preferred_element_type=jnp.float32)
    combine = jax.nn.softmax(logits, axis=-1)
    grad_slot = jnp.einsum(
        "tbs,tbd->bsd",
        combine.astype(jnp.bfloat16),
        grad_out,
        preferred_element_type=jnp.float32,
    ).astype(jnp.bfloat16)
    grad_slot_out = return_grads(grad_slot, owners, me)
    grad_comb = jnp.einsum("tbd,bsd->tbs", grad_out, slot_rows, preferred_element_type=jnp.float32)
    rowdot = jnp.sum(combine * grad_comb, axis=-1, keepdims=True)
    grad_logits = (combine * (grad_comb - rowdot)).astype(jnp.bfloat16)
    param_part = jnp.einsum("tbs,tbd->sd", grad_logits, tokens, preferred_element_type=jnp.float32)
    grad_params = reduce_params(param_part, owners, shards)
    grad_tok = jnp.einsum(
        "tbs,sd->tbd", grad_logits, all_params, preferred_element_type=jnp.float32
    ).astype(jnp.bfloat16)
    return (grad_tok, grad_slot_out, grad_params)


def solution(mesh):
    return jax.shard_map(
        per_device,
        mesh=mesh,
        in_specs=(
            P(None, ("dp", "expert"), None),
            P(None, ("dp", "expert"), None),
            P("expert", "dp", None),
            P("expert", None),
        ),
        out_specs=(P(None, ("dp", "expert"), None), P("expert", "dp", None), P("expert", "dp")),
        check_vma=False,
    )
```

profile of v0, /device:TPU:0, one launch (start us, length us, event | category | flops | bytes accessed | tf_op | source)
XLA Modules:
  0.0 255.6 jit_solution(9286236507647552560)
XLA Ops:
  2.1 2.5 collective-permute-start.1
  6.4 2.6 %collective-permute-start.5 = (bf16[64,256]{1,0:T(8,128)(2,1)S(1)}, bf16[64,256]{1,0:T(8,128)(2,1)S(1)}, u32[]{:S(2)}, u32[]{:S(2)}) collective-permute-start(bf16[64,256]{1,0:T(8,128)(2,1)S(1)} %constant_dynamic-slice_fusion.3), channel_id=1, source_target_pairs={{0,6},{1,7},{2,4},{3,5},{4,2},{5,3},{6,0},{7,1},{8,14},{9,15},{10,... | collective-permute-start | bytes 98312 | tf_op jit(solution)/shard_map/ppermute | solution.py:20
  11.2 2.0 collective-permute-done.6
  15.0 2.6 %collective-permute-start.8 = (bf16[512,256]{1,0:T(8,128)(2,1)S(1)}, bf16[512,256]{1,0:T(8,128)(2,1)}, u32[]{:S(2)}, u32[]{:S(2)}) collective-permute-start(bf16[512,256]{1,0:T(8,128)(2,1)S(1)} %constant_dynamic-update-slice_fusion), channel_id=1, source_target_pairs={{0,16},{8,24},{16,0},{24,8},{1,17},{9,25},{17,1},{25,9},{2,18},{10... | collective-permute-start | bytes 786440 | tf_op jit(solution)/shard_map/ppermute | solution.py:20
  17.8 9.6 %shard_map.68 = (bf16[6,48,1024]{2,1,0:T(8,128)(2,1)}, bf16[6,48,1024]{2,1,0:T(8,128)(2,1)}, bf16[6,48,1024]{2,1,0:T(8,128)(2,1)}, bf16[6,48,1024]{2,1,0:T(8,128...) custom-call(s32[1]{0:T(128)} %bitcast.10.me_ref, ...), custom_call_target="tpu_custom_call" | custom-call | tf_op jit(solution)/shard_map/pallas_call | solution.py:54
  28.1 3.9 %shard_map.67 = (bf16[6,16,1024]{2,1,0:T(8,128)(2,1)}, bf16[6,16,1024]{2,1,0:T(8,128)(2,1)}, bf16[6,16,1024]{2,1,0:T(8,128)(2,1)}, bf16[6,16,1024]{2,1,0:T(8,128...) custom-call(s32[1]{0:T(128)} %bitcast.10.me_ref, ...), custom_call_target="tpu_custom_call" | custom-call | tf_op jit(solution)/shard_map/pallas_call | solution.py:54
  32.3 4.1 %collective-permute-done.8 = bf16[512,256]{1,0:T(8,128)(2,1)} collective-permute-done((bf16[512,256]{1,0:T(8,128)(2,1)S(1)}, bf16[512,256]{1,0:T(8,128)(2,1)}, u32[]{:S(2)}, u32[]{:S(2)}) %collective-permute-start.8) | collective-permute-done | bytes 262176 | tf_op jit(solution)/shard_map/ppermute | solution.py:20
  41.4 6.8 %collective-permute-done.11 = bf16[6,16,1024]{2,1,0:T(8,128)(2,1)S(1)} collective-permute-done((bf16[6,16,1024]{2,1,0:T(8,128)(2,1)}, bf16[6,16,1024]{2,1,0:T(8,128)(2,1)S(1)}, u32[]{:S(2)}, u32[]{:S(2)}) %collective-permute-start.11) | collective-permute-done | bytes 196640 | tf_op jit(solution)/shard_map/ppermute | solution.py:20
  48.2 3.1 %collective-permute-done.12 = bf16[6,16,1024]{2,1,0:T(8,128)(2,1)S(1)} collective-permute-done((bf16[6,16,1024]{2,1,0:T(8,128)(2,1)}, bf16[6,16,1024]{2,1,0:T(8,128)(2,1)S(1)}, u32[]{:S(2)}, u32[]{:S(2)}) %collective-permute-start.12) | collective-permute-done | bytes 196640 | tf_op jit(solution)/shard_map/ppermute | solution.py:20
  52.4 1.9 collective-permute-start.16
  54.3 2.3 fusion.26
  57.5 2.6 %collective-permute-done.15 = bf16[6,16,1024]{2,1,0:T(8,128)(2,1)} collective-permute-done((bf16[6,16,1024]{2,1,0:T(8,128)(2,1)S(1)}, bf16[6,16,1024]{2,1,0:T(8,128)(2,1)}, u32[]{:S(2)}, u32[]{:S(2)}) %collective-permute-start.15) | collective-permute-done | bytes 196640 | tf_op jit(solution)/shard_map/ppermute | solution.py:20
  60.6 3.2 %collective-permute-done.16 = bf16[6,16,1024]{2,1,0:T(8,128)(2,1)} collective-permute-done((bf16[6,16,1024]{2,1,0:T(8,128)(2,1)S(1)}, bf16[6,16,1024]{2,1,0:T(8,128)(2,1)}, u32[]{:S(2)}, u32[]{:S(2)}) %collective-permute-start.16) | collective-permute-done | bytes 196640 | tf_op jit(solution)/shard_map/ppermute | solution.py:20
  66.6 7.2 %convolution_convert_fusion = bf16[6,512,1024]{2,1,0:T(8,128)(2,1)} fusion(bf16[256,6,1024]{2,0,1:T(8,128)(2,1)S(1)} %copy-done, f32[256,6]{0,1:T(8,128)S(1)} %get-tuple-element.123, f32[512,256,6]{1,0,2:T(8,128)} %copy-done.3), kind=kOutput, calls=%fused_computation.1 | convolution fusion | flops 1616119808 | bytes 12589056 | tf_op jit(solution)/shard_map/tbs,tbd->bsd/dot_general | solution.py:153
  73.9 4.1 %fusion.23 = (bf16[6,48,1024]{2,1,0:T(8,128)(2,1)S(1)}, bf16[6,48,1024]{2,1,0:T(8,128)(2,1)S(1)}, bf16[6,48,1024]{2,1,0:T(8,128)(2,1)S(1)}, bf16[6,48,1024]{2,1,...) fusion(bf16[6,512,1024]{2,1,0:T(8,128)(2,1)} %convolution_conve, ...), kind=kLoop, calls=%fused_computation.61 | loop fusion | bytes 9437184 | tf_op jit(solution)/shard_map/slice | solution.py:122
  78.7 23.1 %collective-permute-done.20 = bf16[6,48,1024]{2,1,0:T(8,128)(2,1)} collective-permute-done((bf16[6,48,1024]{2,1,0:T(8,128)(2,1)}, bf16[6,48,1024]{2,1,0:T(8,128)(2,1)}, u32[]{:S(2)}, u32[]{:S(2)}) %collective-permute-start.20) | collective-permute-done | bytes 589856 | tf_op jit(solution)/shard_map/ppermute | solution.py:20
  102.3 12.0 %collective-permute-done.21 = bf16[6,48,1024]{2,1,0:T(8,128)(2,1)} collective-permute-done((bf16[6,48,1024]{2,1,0:T(8,128)(2,1)}, bf16[6,48,1024]{2,1,0:T(8,128)(2,1)}, u32[]{:S(2)}, u32[]{:S(2)}) %collective-permute-start.21) | collective-permute-done | bytes 589856 | tf_op jit(solution)/shard_map/ppermute | solution.py:20
  131.1 3.5 %collective-permute-start.39 = (bf16[512,256]{1,0:T(8,128)(2,1)S(1)}, bf16[512,256]{1,0:T(8,128)(2,1)S(1)}, u32[]{:S(2)}, u32[]{:S(2)}) collective-permute-start(bf16[512,256]{1,0:T(8,128)(2,1)S(1)} %get-tuple-element.111), channel_id=1, source_target_pairs={{0,16},{8,24},{16,0},{24,8},{1,17},{9,25},{17,1},{25,9},{2,18},{10... | collective-permute-start | bytes 786440 | tf_op jit(solution)/shard_map/ppermute | solution.py:20
  134.8 2.5 fusion.24
  137.3 6.5 %collective-permute-done.38 = bf16[512,256]{1,0:T(8,128)(2,1)S(1)} collective-permute-done((bf16[512,256]{1,0:T(8,128)(2,1)S(1)}, bf16[512,256]{1,0:T(8,128)(2,1)S(1)}, u32[]{:S(2)}, u32[]{:S(2)}) %collective-permute-start.38) | collective-permute-done | bytes 262176 | tf_op jit(solution)/shard_map/ppermute | solution.py:20
  143.8 9.2 %collective-permute-done.39 = bf16[512,256]{1,0:T(8,128)(2,1)S(1)} collective-permute-done((bf16[512,256]{1,0:T(8,128)(2,1)S(1)}, bf16[512,256]{1,0:T(8,128)(2,1)S(1)}, u32[]{:S(2)}, u32[]{:S(2)}) %collective-permute-start.39) | collective-permute-done | bytes 262176 | tf_op jit(solution)/shard_map/ppermute | solution.py:20
  155.9 3.1 %collective-permute-done.25.refs_2_ = bf16[6,16,1024]{2,1,0:T(8,128)(2,1)S(1)} collective-permute-done((bf16[6,16,1024]{2,1,0:T(8,128)(2,1)S(1)}, bf16[6,16,1024]{2,1,0:T(8,128)(2,1)S(1)}, u32[]{:S(2)}, u32[]{:S(2)}) %collective-permute-start.25) | collective-permute-done | bytes 196640 | tf_op jit(solution)/shard_map/ppermute | solution.py:20
  163.5 11.1 %collective-permute-done.33.refs_3_ = bf16[6,48,1024]{2,1,0:T(8,128)(2,1)S(1)} collective-permute-done((bf16[6,48,1024]{2,1,0:T(8,128)(2,1)S(1)}, bf16[6,48,1024]{2,1,0:T(8,128)(2,1)S(1)}, u32[]{:S(2)}, u32[]{:S(2)}) %collective-permute-start.33) | collective-permute-done | bytes 589856 | tf_op jit(solution)/shard_map/ppermute | solution.py:20
  175.0 25.6 %collective-permute-done.34.refs_4_ = bf16[6,48,1024]{2,1,0:T(8,128)(2,1)S(1)} collective-permute-done((bf16[6,48,1024]{2,1,0:T(8,128)(2,1)S(1)}, bf16[6,48,1024]{2,1,0:T(8,128)(2,1)S(1)}, u32[]{:S(2)}, u32[]{:S(2)}) %collective-permute-start.34) | collective-permute-done | bytes 589856 | tf_op jit(solution)/shard_map/ppermute | solution.py:20
  200.9 11.5 %collective-permute-done.35.refs_5_ = bf16[6,48,1024]{2,1,0:T(8,128)(2,1)S(1)} collective-permute-done((bf16[6,48,1024]{2,1,0:T(8,128)(2,1)S(1)}, bf16[6,48,1024]{2,1,0:T(8,128)(2,1)S(1)}, u32[]{:S(2)}, u32[]{:S(2)}) %collective-permute-start.35) | collective-permute-done | bytes 589856 | tf_op jit(solution)/shard_map/ppermute | solution.py:20
  215.2 2.0 collective-permute-start.47
  217.2 3.5 %convolution_convert_fusion.1 = bf16[256,6,1024]{2,0,1:T(8,128)(2,1)} fusion(bf16[256,6,512]{0,2,1:T(8,128)(2,1)S(1)} %fusion.3, bf16[512,256]{1,0:T(8,128)(2,1)S(1)} %copy-done.13, bf16[512,256]{1,0:T(8,128)(2,1)S(1)} %copy-done.15, bf16[512,256]{1,0:T(8,128)(2,1)S(1)} %copy-done.17, bf16[512,256]{1,0:T(8,128)(2,1)S(1)} %get-tuple-element.112), kind=kOutput, calls=%fused_computation.11 | convolution fusion | flops 1616379904 | bytes 5767168 | tf_op jit(solution)/shard_map/tbs,sd->tbd/dot_general | solution.py:165
  220.8 9.5 %shard_map.69.refs_8_ = bf16[64,48,1024]{2,1,0:T(8,128)(2,1)} custom-call(s32[1]{0:T(128)} %bitcast.10.me_ref, bf16[6,48,1024]{2,1,0:T(8,128)(2,1)} %get-tuple-element.100.refs_0_, bf16[6,48,1024]{2,1,0:T(8,128)(2,1)} %copy-done.4, bf16[6,48,1024]{2,1,0:T(8,128)(2,1)} %copy-done.5, bf16[6,48,1024]{2,1,0:T(8,128)(2,1)} %copy-done.6, ...), custom_call_target="tpu_custom_call" | custom-call | tf_op jit(solution)/shard_map/pallas_call | solution.py:84
  233.7 1.9 collective-permute-start.30
  237.4 10.0 %collective-permute-done.27.refs_4_ = bf16[6,16,1024]{2,1,0:T(8,128)(2,1)S(1)} collective-permute-done((bf16[6,16,1024]{2,1,0:T(8,128)(2,1)S(1)}, bf16[6,16,1024]{2,1,0:T(8,128)(2,1)S(1)}, u32[]{:S(2)}, u32[]{:S(2)}) %collective-permute-start.27) | collective-permute-done | bytes 196640 | tf_op jit(solution)/shard_map/ppermute | solution.py:20
  247.4 2.5 collective-permute-done.28.refs_5_
  251.4 4.0 %shard_map.70 = bf16[64,48,1024]{2,1,0:T(8,128)(2,1)} custom-call(s32[1]{0:T(128)} %bitcast.10.me_ref, bf16[6,16,1024]{2,1,0:T(8,128)(2,1)} %get-tuple-element.108.refs_0_, bf16[6,16,1024]{2,1,0:T(8,128)(2,1)} %copy-done.34, bf16[6,16,1024]{2,1,0:T(8,128)(2,1)} %copy-done.35, bf16[6,16,1024]{2,1,0:T(8,128)(2,1)} %copy-done.36, ...), custom_call_target="tpu_custom_call", output_to_operand_aliasing={{}: (9, {})} | custom-call | tf_op jit(solution)/shard_map/pallas_call | solution.py:84
  (202 shorter events, 53.9 us)
Async XLA Ops:
  13.3 18.7 %collective-permute-start.7 = (bf16[512,256]{1,0:T(8,128)(2,1)S(1)}, bf16[512,256]{1,0:T(8,128)(2,1)}, u32[]{:S(2)}, u32[]{:S(2)}) collective-permute-start(bf16[512,256]{1,0:T(8,128)(2,1)S(1)} %constant_dynamic-update-slice_fusion), channel_id=1, source_target_pairs={{0,8},{8,0},{16,24},{24,16},{1,9},{9,1},{17,25},{25,17},{2,10},{10... | collective-permute-start | bytes 786440 | tf_op jit(solution)/shard_map/ppermute | solution.py:20
  15.0 21.4 %collective-permute-start.8 = (bf16[512,256]{1,0:T(8,128)(2,1)S(1)}, bf16[512,256]{1,0:T(8,128)(2,1)}, u32[]{:S(2)}, u32[]{:S(2)}) collective-permute-start(bf16[512,256]{1,0:T(8,128)(2,1)S(1)} %constant_dynamic-update-slice_fusion), channel_id=1, source_target_pairs={{0,16},{8,24},{16,0},{24,8},{1,17},{9,25},{17,1},{25,9},{2,18},{10... | collective-permute-start | bytes 786440 | tf_op jit(solution)/shard_map/ppermute | solution.py:20
  17.5 19.4 %collective-permute-start.9 = (bf16[512,256]{1,0:T(8,128)(2,1)S(1)}, bf16[512,256]{1,0:T(8,128)(2,1)}, u32[]{:S(2)}, u32[]{:S(2)}) collective-permute-start(bf16[512,256]{1,0:T(8,128)(2,1)S(1)} %constant_dynamic-update-slice_fusion), channel_id=1, source_target_pairs={{0,24},{8,16},{16,8},{24,0},{1,25},{9,17},{17,9},{25,1},{2,26},{10... | collective-permute-start | bytes 786440 | tf_op jit(solution)/shard_map/ppermute | solution.py:20
  27.4 36.8 %collective-permute-start.17 = (bf16[6,48,1024]{2,1,0:T(8,128)(2,1)}, bf16[6,48,1024]{2,1,0:T(8,128)(2,1)}, u32[]{:S(2)}, u32[]{:S(2)}) collective-permute-start(bf16[6,48,1024]{2,1,0:T(8,128)(2,1)} %get-tuple-element.68), channel_id=1, source_target_pairs={{0,1},{1,0},{2,3},{3,2},{4,5},{5,4},{6,7},{7,6},{8,9},{9,8},{10,11... | collective-permute-start | bytes 1769480 | tf_op jit(solution)/shard_map/ppermute | solution.py:20
  27.5 38.2 %collective-permute-start.18 = (bf16[6,48,1024]{2,1,0:T(8,128)(2,1)}, bf16[6,48,1024]{2,1,0:T(8,128)(2,1)}, u32[]{:S(2)}, u32[]{:S(2)}) collective-permute-start(bf16[6,48,1024]{2,1,0:T(8,128)(2,1)} %get-tuple-element.69), channel_id=1, source_target_pairs={{0,2},{1,3},{2,0},{3,1},{4,6},{5,7},{6,4},{7,5},{8,10},{9,11},{10,... | collective-permute-start | bytes 1769480 | tf_op jit(solution)/shard_map/ppermute | solution.py:20
  36.4 11.8 %collective-permute-start.11 = (bf16[6,16,1024]{2,1,0:T(8,128)(2,1)}, bf16[6,16,1024]{2,1,0:T(8,128)(2,1)S(1)}, u32[]{:S(2)}, u32[]{:S(2)}) collective-permute-start(bf16[6,16,1024]{2,1,0:T(8,128)(2,1)} %get-tuple-element.61), channel_id=1, source_target_pairs={{0,2},{1,3},{2,0},{3,1},{4,6},{5,7},{6,4},{7,5},{8,10},{9,11},{10,... | collective-permute-start | bytes 589832 | tf_op jit(solution)/shard_map/ppermute | solution.py:20
  36.9 14.4 %collective-permute-start.12 = (bf16[6,16,1024]{2,1,0:T(8,128)(2,1)}, bf16[6,16,1024]{2,1,0:T(8,128)(2,1)S(1)}, u32[]{:S(2)}, u32[]{:S(2)}) collective-permute-start(bf16[6,16,1024]{2,1,0:T(8,128)(2,1)} %get-tuple-element.62), channel_id=1, source_target_pairs={{0,3},{1,2},{2,1},{3,0},{4,7},{5,6},{6,5},{7,4},{8,11},{9,10},{10,... | collective-permute-start | bytes 589832 | tf_op jit(solution)/shard_map/ppermute | solution.py:20
  38.3 14.1 %collective-permute-start.13 = (bf16[6,16,1024]{2,1,0:T(8,128)(2,1)S(1)}, bf16[6,16,1024]{2,1,0:T(8,128)(2,1)S(1)}, u32[]{:S(2)}, u32[]{:S(2)}) collective-permute-start(bf16[6,16,1024]{2,1,0:T(8,128)(2,1)S(1)} %copy-done.46), channel_id=1, source_target_pairs={{0,4},{1,5},{2,6},{3,7},{4,0},{5,1},{6,2},{7,3},{8,12},{9,13},{10,... | collective-permute-start | bytes 589832 | tf_op jit(solution)/shard_map/ppermute | solution.py:20
  57.2 20.8 %collective-permute-start.19 = (bf16[6,48,1024]{2,1,0:T(8,128)(2,1)}, bf16[6,48,1024]{2,1,0:T(8,128)(2,1)}, u32[]{:S(2)}, u32[]{:S(2)}) collective-permute-start(bf16[6,48,1024]{2,1,0:T(8,128)(2,1)} %get-tuple-element.70), channel_id=1, source_target_pairs={{0,3},{1,2},{2,1},{3,0},{4,7},{5,6},{6,5},{7,4},{8,11},{9,10},{10,... | collective-permute-start | bytes 1769480 | tf_op jit(solution)/shard_map/ppermute | solution.py:20
  60.1 41.7 %collective-permute-start.20 = (bf16[6,48,1024]{2,1,0:T(8,128)(2,1)}, bf16[6,48,1024]{2,1,0:T(8,128)(2,1)}, u32[]{:S(2)}, u32[]{:S(2)}) collective-permute-start(bf16[6,48,1024]{2,1,0:T(8,128)(2,1)} %get-tuple-element.71), channel_id=1, source_target_pairs={{0,4},{1,5},{2,6},{3,7},{4,0},{5,1},{6,2},{7,3},{8,12},{9,13},{10,... | collective-permute-start | bytes 1769480 | tf_op jit(solution)/shard_map/ppermute | solution.py:20
  63.8 50.6 %collective-permute-start.21 = (bf16[6,48,1024]{2,1,0:T(8,128)(2,1)}, bf16[6,48,1024]{2,1,0:T(8,128)(2,1)}, u32[]{:S(2)}, u32[]{:S(2)}) collective-permute-start(bf16[6,48,1024]{2,1,0:T(8,128)(2,1)} %get-tuple-element.72), channel_id=1, source_target_pairs={{0,5},{1,4},{2,7},{3,6},{4,1},{5,0},{6,3},{7,2},{8,13},{9,12},{10,... | collective-permute-start | bytes 1769480 | tf_op jit(solution)/shard_map/ppermute | solution.py:20
  64.2 50.2 %collective-permute-start.22 = (bf16[6,48,1024]{2,1,0:T(8,128)(2,1)}, bf16[6,48,1024]{2,1,0:T(8,128)(2,1)}, u32[]{:S(2)}, u32[]{:S(2)}) collective-permute-start(bf16[6,48,1024]{2,1,0:T(8,128)(2,1)} %get-tuple-element.73), channel_id=1, source_target_pairs={{0,6},{1,7},{2,4},{3,5},{4,2},{5,3},{6,0},{7,1},{8,14},{9,15},{10,... | collective-permute-start | bytes 1769480 | tf_op jit(solution)/shard_map/ppermute | solution.py:20
  65.7 48.7 %collective-permute-start.23 = (bf16[6,48,1024]{2,1,0:T(8,128)(2,1)}, bf16[6,48,1024]{2,1,0:T(8,128)(2,1)}, u32[]{:S(2)}, u32[]{:S(2)}) collective-permute-start(bf16[6,48,1024]{2,1,0:T(8,128)(2,1)} %get-tuple-element.74), channel_id=1, source_target_pairs={{0,7},{1,6},{2,5},{3,4},{4,3},{5,2},{6,1},{7,0},{8,15},{9,14},{10,... | collective-permute-start | bytes 1769480 | tf_op jit(solution)/shard_map/ppermute | solution.py:20
  78.0 83.0 %collective-permute-start.31 = (bf16[6,48,1024]{2,1,0:T(8,128)(2,1)S(1)}, bf16[6,48,1024]{2,1,0:T(8,128)(2,1)S(1)}, u32[]{:S(2)}, u32[]{:S(2)}) collective-permute-start(bf16[6,48,1024]{2,1,0:T(8,128)(2,1)S(1)} %get-tuple-element.99), channel_id=1, source_target_pairs={{0,1},{1,0},{2,3},{3,2},{4,5},{5,4},{6,7},{7,6},{8,9},{9,8},{10,11... | collective-permute-start | bytes 1769480 | tf_op jit(solution)/shard_map/ppermute | solution.py:20
  101.8 60.7 %collective-permute-start.32 = (bf16[6,48,1024]{2,1,0:T(8,128)(2,1)S(1)}, bf16[6,48,1024]{2,1,0:T(8,128)(2,1)S(1)}, u32[]{:S(2)}, u32[]{:S(2)}) collective-permute-start(bf16[6,48,1024]{2,1,0:T(8,128)(2,1)S(1)} %get-tuple-element.98), channel_id=1, source_target_pairs={{0,2},{1,3},{2,0},{3,1},{4,6},{5,7},{6,4},{7,5},{8,10},{9,11},{10,... | collective-permute-start | bytes 1769480 | tf_op jit(solution)/shard_map/ppermute | solution.py:20
  130.4 13.5 %collective-permute-start.38 = (bf16[512,256]{1,0:T(8,128)(2,1)S(1)}, bf16[512,256]{1,0:T(8,128)(2,1)S(1)}, u32[]{:S(2)}, u32[]{:S(2)}) collective-permute-start(bf16[512,256]{1,0:T(8,128)(2,1)S(1)} %get-tuple-element.109), channel_id=1, source_target_pairs={{0,8},{8,0},{16,24},{24,16},{1,9},{9,1},{17,25},{25,17},{2,10},{10... | collective-permute-start | bytes 786440 | tf_op jit(solution)/shard_map/ppermute | solution.py:20
  131.1 21.9 %collective-permute-start.39 = (bf16[512,256]{1,0:T(8,128)(2,1)S(1)}, bf16[512,256]{1,0:T(8,128)(2,1)S(1)}, u32[]{:S(2)}, u32[]{:S(2)}) collective-permute-start(bf16[512,256]{1,0:T(8,128)(2,1)S(1)} %get-tuple-element.111), channel_id=1, source_target_pairs={{0,16},{8,24},{16,0},{24,8},{1,17},{9,25},{17,1},{25,9},{2,18},{10... | collective-permute-start | bytes 786440 | tf_op jit(solution)/shard_map/ppermute | solution.py:20
  134.6 19.0 %collective-permute-start.40 = (bf16[512,256]{1,0:T(8,128)(2,1)S(1)}, bf16[512,256]{1,0:T(8,128)(2,1)S(1)}, u32[]{:S(2)}, u32[]{:S(2)}) collective-permute-start(bf16[512,256]{1,0:T(8,128)(2,1)S(1)} %get-tuple-element.110), channel_id=1, source_target_pairs={{0,24},{8,16},{16,8},{24,0},{1,25},{9,17},{17,9},{25,1},{2,26},{10... | collective-permute-start | bytes 786440 | tf_op jit(solution)/shard_map/ppermute | solution.py:20
  159.1 15.6 %collective-permute-start.33 = (bf16[6,48,1024]{2,1,0:T(8,128)(2,1)S(1)}, bf16[6,48,1024]{2,1,0:T(8,128)(2,1)S(1)}, u32[]{:S(2)}, u32[]{:S(2)}) collective-permute-start(bf16[6,48,1024]{2,1,0:T(8,128)(2,1)S(1)} %get-tuple-element.97), channel_id=1, source_target_pairs={{0,3},{1,2},{2,1},{3,0},{4,7},{5,6},{6,5},{7,4},{8,11},{9,10},{10,... | collective-permute-start | bytes 1769480 | tf_op jit(solution)/shard_map/ppermute | solution.py:20
  159.1 41.5 %collective-permute-start.34 = (bf16[6,48,1024]{2,1,0:T(8,128)(2,1)S(1)}, bf16[6,48,1024]{2,1,0:T(8,128)(2,1)S(1)}, u32[]{:S(2)}, u32[]{:S(2)}) collective-permute-start(bf16[6,48,1024]{2,1,0:T(8,128)(2,1)S(1)} %get-tuple-element.96), channel_id=1, source_target_pairs={{0,4},{1,5},{2,6},{3,7},{4,0},{5,1},{6,2},{7,3},{8,12},{9,13},{10,... | collective-permute-start | bytes 1769480 | tf_op jit(solution)/shard_map/ppermute | solution.py:20
  159.6 52.7 %collective-permute-start.35 = (bf16[6,48,1024]{2,1,0:T(8,128)(2,1)S(1)}, bf16[6,48,1024]{2,1,0:T(8,128)(2,1)S(1)}, u32[]{:S(2)}, u32[]{:S(2)}) collective-permute-start(bf16[6,48,1024]{2,1,0:T(8,128)(2,1)S(1)} %get-tuple-element.95), channel_id=1, source_target_pairs={{0,5},{1,4},{2,7},{3,6},{4,1},{5,0},{6,3},{7,2},{8,13},{9,12},{10,... | collective-permute-start | bytes 1769480 | tf_op jit(solution)/shard_map/ppermute | solution.py:20
  161.0 52.3 %collective-permute-start.36 = (bf16[6,48,1024]{2,1,0:T(8,128)(2,1)S(1)}, bf16[6,48,1024]{2,1,0:T(8,128)(2,1)S(1)}, u32[]{:S(2)}, u32[]{:S(2)}) collective-permute-start(bf16[6,48,1024]{2,1,0:T(8,128)(2,1)S(1)} %get-tuple-element.94), channel_id=1, source_target_pairs={{0,6},{1,7},{2,4},{3,5},{4,2},{5,3},{6,0},{7,1},{8,14},{9,15},{10,... | collective-permute-start | bytes 1769480 | tf_op jit(solution)/shard_map/ppermute | solution.py:20
  162.5 51.8 %collective-permute-start.37 = (bf16[6,48,1024]{2,1,0:T(8,128)(2,1)S(1)}, bf16[6,48,1024]{2,1,0:T(8,128)(2,1)S(1)}, u32[]{:S(2)}, u32[]{:S(2)}) collective-permute-start(bf16[6,48,1024]{2,1,0:T(8,128)(2,1)S(1)} %get-tuple-element.93), channel_id=1, source_target_pairs={{0,7},{1,6},{2,5},{3,4},{4,3},{5,2},{6,1},{7,0},{8,15},{9,14},{10,... | collective-permute-start | bytes 1769480 | tf_op jit(solution)/shard_map/ppermute | solution.py:20
  174.7 55.6 %collective-permute-start.43 = (bf16[64,256]{1,0:T(8,128)(2,1)S(1)}, bf16[64,256]{1,0:T(8,128)(2,1)S(1)}, u32[]{:S(2)}, u32[]{:S(2)}) collective-permute-start(bf16[64,256]{1,0:T(8,128)(2,1)S(1)} %get-tuple-element.121), channel_id=1, source_target_pairs={{0,3},{1,2},{2,1},{3,0},{4,7},{5,6},{6,5},{7,4},{8,11},{9,10},{10,... | collective-permute-start | bytes 98312 | tf_op jit(solution)/shard_map/ppermute | solution.py:20
  200.6 30.6 %collective-permute-start.44 = (bf16[64,256]{1,0:T(8,128)(2,1)S(1)}, bf16[64,256]{1,0:T(8,128)(2,1)S(1)}, u32[]{:S(2)}, u32[]{:S(2)}) collective-permute-start(bf16[64,256]{1,0:T(8,128)(2,1)S(1)} %get-tuple-element.120), channel_id=1, source_target_pairs={{0,4},{1,5},{2,6},{3,7},{4,0},{5,1},{6,2},{7,3},{8,12},{9,13},{10,... | collective-permute-start | bytes 98312 | tf_op jit(solution)/shard_map/ppermute | solution.py:20
  212.4 19.2 %collective-permute-start.45 = (bf16[64,256]{1,0:T(8,128)(2,1)}, bf16[64,256]{1,0:T(8,128)(2,1)S(1)}, u32[]{:S(2)}, u32[]{:S(2)}) collective-permute-start(bf16[64,256]{1,0:T(8,128)(2,1)} %get-tuple-element.119), channel_id=1, source_target_pairs={{0,5},{1,4},{2,7},{3,6},{4,1},{5,0},{6,3},{7,2},{8,13},{9,12},{10,... | collective-permute-start | bytes 98312 | tf_op jit(solution)/shard_map/ppermute | solution.py:20
  213.3 19.4 %collective-permute-start.46 = (bf16[64,256]{1,0:T(8,128)(2,1)}, bf16[64,256]{1,0:T(8,128)(2,1)S(1)}, u32[]{:S(2)}, u32[]{:S(2)}) collective-permute-start(bf16[64,256]{1,0:T(8,128)(2,1)} %get-tuple-element.118), channel_id=1, source_target_pairs={{0,6},{1,7},{2,4},{3,5},{4,2},{5,3},{6,0},{7,1},{8,14},{9,15},{10,... | collective-permute-start | bytes 98312 | tf_op jit(solution)/shard_map/ppermute | solution.py:20
  215.2 18.5 %collective-permute-start.47 = (bf16[64,256]{1,0:T(8,128)(2,1)}, bf16[64,256]{1,0:T(8,128)(2,1)S(1)}, u32[]{:S(2)}, u32[]{:S(2)}) collective-permute-start(bf16[64,256]{1,0:T(8,128)(2,1)} %get-tuple-element.117), channel_id=1, source_target_pairs={{0,7},{1,6},{2,5},{3,4},{4,3},{5,2},{6,1},{7,0},{8,15},{9,14},{10,... | collective-permute-start | bytes 98312 | tf_op jit(solution)/shard_map/ppermute | solution.py:20
  231.2 16.2 %collective-permute-start.27 = (bf16[6,16,1024]{2,1,0:T(8,128)(2,1)S(1)}, bf16[6,16,1024]{2,1,0:T(8,128)(2,1)S(1)}, u32[]{:S(2)}, u32[]{:S(2)}) collective-permute-start(bf16[6,16,1024]{2,1,0:T(8,128)(2,1)S(1)} %copy-done.21), channel_id=1, source_target_pairs={{0,4},{1,5},{2,6},{3,7},{4,0},{5,1},{6,2},{7,3},{8,12},{9,13},{10,... | collective-permute-start | bytes 589832 | tf_op jit(solution)/shard_map/ppermute | solution.py:20
  231.6 18.3 %collective-permute-start.28 = (bf16[6,16,1024]{2,1,0:T(8,128)(2,1)S(1)}, bf16[6,16,1024]{2,1,0:T(8,128)(2,1)S(1)}, u32[]{:S(2)}, u32[]{:S(2)}) collective-permute-start(bf16[6,16,1024]{2,1,0:T(8,128)(2,1)S(1)} %copy-done.20), channel_id=1, source_target_pairs={{0,5},{1,4},{2,7},{3,6},{4,1},{5,0},{6,3},{7,2},{8,13},{9,12},{10,... | collective-permute-start | bytes 589832 | tf_op jit(solution)/shard_map/ppermute | solution.py:20
  232.7 17.2 %collective-permute-start.29 = (bf16[6,16,1024]{2,1,0:T(8,128)(2,1)S(1)}, bf16[6,16,1024]{2,1,0:T(8,128)(2,1)S(1)}, u32[]{:S(2)}, u32[]{:S(2)}) collective-permute-start(bf16[6,16,1024]{2,1,0:T(8,128)(2,1)S(1)} %copy-done.19), channel_id=1, source_target_pairs={{0,6},{1,7},{2,4},{3,5},{4,2},{5,3},{6,0},{7,1},{8,14},{9,15},{10,... | collective-permute-start | bytes 589832 | tf_op jit(solution)/shard_map/ppermute | solution.py:20
  233.7 16.2 %collective-permute-start.30 = (bf16[6,16,1024]{2,1,0:T(8,128)(2,1)S(1)}, bf16[6,16,1024]{2,1,0:T(8,128)(2,1)S(1)}, u32[]{:S(2)}, u32[]{:S(2)}) collective-permute-start(bf16[6,16,1024]{2,1,0:T(8,128)(2,1)S(1)} %copy-done.18), channel_id=1, source_target_pairs={{0,7},{1,6},{2,5},{3,4},{4,3},{5,2},{6,1},{7,0},{8,15},{9,14},{10,... | collective-permute-start | bytes 589832 | tf_op jit(solution)/shard_map/ppermute | solution.py:20
  (63 other events, 1124.3 us)
where the time goes:
time: 257 us; the launch traced here: 256 us
  waiting for transfers between devices  140 us (54%)
  starting transfers between devices  43.3 us (17%)
  Pallas kernels  27.1 us (11%)
  local copies, waits for them, and re-layouts  22.9 us (9%)
  matrix products  16.2 us (6%)
  other arithmetic  4.79 us (2%)
    ppermute x48, waiting for transfers between devices, trade(): return lax.ppermute(x, axis, partners(lax.axis_size(axis), step))  140 us
    ppermute x48, starting transfers between devices, trade(): return lax.ppermute(x, axis, partners(lax.axis_size(axis), step))  43.3 us
    pallas_call x2, Pallas kernels, split_slots(): pl.pallas_call(split_kernel, out_shape=[jax.ShapeDtypeStruct((images, uni...  13.6 us
    pallas_call x2, Pallas kernels, join_slots(): pl.pallas_call(join_kernel, out_shape=jax.ShapeDtypeStruct((own_slots, ow...  13.6 us
    unnamed x116, local copies, waits for them, and re-layouts  13.4 us
    dot_general x1, matrix products, per_device(): jnp.einsum('tbs,tbd->bsd', combine.astype(jnp.bfloat16), grad_out, prefer...  7.23 us
    slice x2, local copies, waits for them, and re-layouts, return_grads(): block = grad_slot[:, at:at + units * unit]  6.64 us
  transfers between devices with their start and end apart: 48, of which 19 were waited for; matrix products, arithmetic and copies ran while one was open for 15% of the time, Pallas kernels for 9%

commit v1 on v0

--- a/solution.py
+++ b/solution.py
@@ -7,7 +7,7 @@
 
 
 UNITS = 4
-OUT_UNITS = (1, 3)
+OUT_UNITS = (2, 2)
 BACK_UNITS = (3, 1)
 LANES = 256
 
@@ -31,7 +31,8 @@
     part = jnp.concatenate(lax.optimization_barrier(blocks), axis=0)
     parts = [part]
     for j in range(1, shards):
-        parts.append(trade(part, "dp", j))
+        low = j & -j
+        parts.append(trade(parts[j ^ low], "dp", low))
     parts = jnp.stack(lax.optimization_barrier(parts))
     return jnp.concatenate(
         [lax.dynamic_index_in_dim(parts, j ^ shard, 0, keepdims=False) for j in range(shards)],
@@ -134,7 +135,8 @@
     total = lax.dynamic_slice_in_dim(param_part, shard * cols, cols, axis=1)
     for j in range(1, shards):
         block = lax.dynamic_slice_in_dim(low, (shard ^ j) * cols, cols, axis=1)
-        total = total + trade(block, "dp", j).astype(jnp.float32)
+        block = trade(block, "dp", j)
+        total = total + block.astype(jnp.float32)
     low = total.astype(jnp.bfloat16)
     owned = total[:own_slots]
     for k in range(1, owners):

time: 257 us -> 257 us (level)
  waiting for transfers between devices: 140 us -> 125 us
  starting transfers between devices: 43.3 us -> 48.6 us
  local copies, waits for them, and re-layouts: 22.9 us -> 28.2 us
  matrix products: 16.2 us -> 20.2 us
    ppermute x48, waiting for transfers between devices: 140 us -> 125 us  [trade(): return lax.ppermute(x, axis, partners(lax.axis_size(axis), step))]
    unnamed x116 -> x74, local copies, waits for them, and re-layouts: 13.4 us -> 22.8 us
    ppermute x48, starting transfers between devices: 43.3 us -> 48.6 us  [trade(): return lax.ppermute(x, axis, partners(lax.axis_size(axis), step))]
    slice x2, local copies, waits for them, and re-layouts: 6.64 us -> 2.61 us  [return_grads(): block = grad_slot[:, at:at + units * unit]]
    dot_general x1, matrix products: 1.88 us -> 5.74 us  [per_device(): jnp.einsum('tbd,bsd->tbs', grad_out, slot_rows, preferred_element_type=jn...]
  transfers between devices with their start and end apart: 48 -> 48, of which waited for: 19 -> 16; matrix products, arithmetic and copies ran while one was open for 15% -> 11% of each run, Pallas kernels for 9% -> 9%
where the time goes in v1:
time: 257 us; the launch traced here: 255 us
  waiting for transfers between devices  125 us (49%)
  starting transfers between devices  48.6 us (19%)
  local copies, waits for them, and re-layouts  28.2 us (11%)
  Pallas kernels  27.2 us (11%)
  matrix products  20.2 us (8%)
  other arithmetic  5.24 us (2%)
    ppermute x48, waiting for transfers between devices, trade(): return lax.ppermute(x, axis, partners(lax.axis_size(axis), step))  125 us
    ppermute x48, starting transfers between devices, trade(): return lax.ppermute(x, axis, partners(lax.axis_size(axis), step))  48.6 us
    unnamed x74, local copies, waits for them, and re-layouts  22.8 us
    pallas_call x2, Pallas kernels, split_slots(): pl.pallas_call(split_kernel, out_shape=[jax.ShapeDtypeStruct((images, uni...  13.8 us
    pallas_call x2, Pallas kernels, join_slots(): pl.pallas_call(join_kernel, out_shape=jax.ShapeDtypeStruct((own_slots, ow...  13.5 us
    dot_general x1, matrix products, per_device(): jnp.einsum('tbs,tbd->bsd', combine.astype(jnp.bfloat16), grad_out, prefer...  7.33 us
    dot_general x1, matrix products, per_device(): jnp.einsum('tbd,bsd->tbs', grad_out, slot_rows, preferred_element_type=jn...  5.74 us
  transfers between devices with their start and end apart: 48, of which 16 were waited for; matrix products, arithmetic and copies ran while one was open for 11% of the time, Pallas kernels for 9%

profile of v1, /device:TPU:0, one launch (start us, length us, event | category | flops | bytes accessed | tf_op | source)
XLA Modules:
  0.0 255.1 jit_solution(4932040679992174803)
XLA Ops:
  2.1 2.5 collective-permute-start.1
  6.4 2.6 %collective-permute-start.5 = (bf16[64,256]{1,0:T(8,128)(2,1)S(1)}, bf16[64,256]{1,0:T(8,128)(2,1)S(1)}, u32[]{:S(2)}, u32[]{:S(2)}) collective-permute-start(bf16[64,256]{1,0:T(8,128)(2,1)S(1)} %constant_dynamic-slice_fusion.3), channel_id=1, source_target_pairs={{0,6},{1,7},{2,4},{3,5},{4,2},{5,3},{6,0},{7,1},{8,14},{9,15},{10,... | collective-permute-start | bytes 98312 | tf_op jit(solution)/shard_map/ppermute | solution.py:20
  9.2 6.8 %shard_map.67 = (bf16[6,32,1024]{2,1,0:T(8,128)(2,1)}, bf16[6,32,1024]{2,1,0:T(8,128)(2,1)}, bf16[6,32,1024]{2,1,0:T(8,128)(2,1)}, bf16[6,32,1024]{2,1,0:T(8,128...) custom-call(s32[1]{0:T(128)} %bitcast.10.me_ref, ...), custom_call_target="tpu_custom_call" | custom-call | tf_op jit(solution)/shard_map/pallas_call | solution.py:55
  24.4 2.6 %collective-permute-start.8 = (bf16[512,256]{1,0:T(8,128)(2,1)}, bf16[512,256]{1,0:T(8,128)(2,1)}, u32[]{:S(2)}, u32[]{:S(2)}) collective-permute-start(bf16[512,256]{1,0:T(8,128)(2,1)} %constant_dynamic-update-slice_fusion), channel_id=1, source_target_pairs={{0,16},{8,24},{16,0},{24,8},{1,17},{9,25},{17,1},{25,9},{2,18},{10... | collective-permute-start | bytes 786440 | tf_op jit(solution)/shard_map/ppermute | solution.py:20
  27.0 7.0 %shard_map.68 = (bf16[6,32,1024]{2,1,0:T(8,128)(2,1)}, bf16[6,32,1024]{2,1,0:T(8,128)(2,1)}, bf16[6,32,1024]{2,1,0:T(8,128)(2,1)}, bf16[6,32,1024]{2,1,0:T(8,128...) custom-call(s32[1]{0:T(128)} %bitcast.10.me_ref, ...), custom_call_target="tpu_custom_call" | custom-call | tf_op jit(solution)/shard_map/pallas_call | solution.py:55
  34.0 5.8 %collective-permute-done.8 = bf16[512,256]{1,0:T(8,128)(2,1)} collective-permute-done((bf16[512,256]{1,0:T(8,128)(2,1)}, bf16[512,256]{1,0:T(8,128)(2,1)}, u32[]{:S(2)}, u32[]{:S(2)}) %collective-permute-start.8) | collective-permute-done | bytes 262176 | tf_op jit(solution)/shard_map/ppermute | solution.py:20
  39.8 2.0 collective-permute-start.15
  44.3 23.6 %collective-permute-done.14 = bf16[6,32,1024]{2,1,0:T(8,128)(2,1)} collective-permute-done((bf16[6,32,1024]{2,1,0:T(8,128)(2,1)}, bf16[6,32,1024]{2,1,0:T(8,128)(2,1)}, u32[]{:S(2)}, u32[]{:S(2)}) %collective-permute-start.14) | collective-permute-done | bytes 393248 | tf_op jit(solution)/shard_map/ppermute | solution.py:20
  73.2 6.4 %collective-permute-done.19 = bf16[6,32,1024]{2,1,0:T(8,128)(2,1)} collective-permute-done((bf16[6,32,1024]{2,1,0:T(8,128)(2,1)}, bf16[6,32,1024]{2,1,0:T(8,128)(2,1)}, u32[]{:S(2)}, u32[]{:S(2)}) %collective-permute-start.19) | collective-permute-done | bytes 393248 | tf_op jit(solution)/shard_map/ppermute | solution.py:20
  80.0 17.9 %collective-permute-done.20 = bf16[6,32,1024]{2,1,0:T(8,128)(2,1)} collective-permute-done((bf16[6,32,1024]{2,1,0:T(8,128)(2,1)}, bf16[6,32,1024]{2,1,0:T(8,128)(2,1)}, u32[]{:S(2)}, u32[]{:S(2)}) %collective-permute-start.20) | collective-permute-done | bytes 393248 | tf_op jit(solution)/shard_map/ppermute | solution.py:20
  99.4 6.6 %collective-permute-done.21 = bf16[6,32,1024]{2,1,0:T(8,128)(2,1)} collective-permute-done((bf16[6,32,1024]{2,1,0:T(8,128)(2,1)}, bf16[6,32,1024]{2,1,0:T(8,128)(2,1)}, u32[]{:S(2)}, u32[]{:S(2)}) %collective-permute-start.21) | collective-permute-done | bytes 393248 | tf_op jit(solution)/shard_map/ppermute | solution.py:20
  121.6 2.7 %copy-done.21 = bf16[6,512,1024]{2,1,0:T(8,128)(2,1)} copy-done((bf16[6,512,1024]{2,1,0:T(8,128)(2,1)}, bf16[6,512,1024]{2,1,0:T(8,128)(2,1)S(1)}, u32[]{:S(2)}) %copy-start.21) | copy-done | bytes 6291480
  125.6 1.8 fusion.9
  127.5 2.7 %fusion.26 = (f32[256,6]{0,1:T(8,128)S(1)}, f32[256,6,512]{0,2,1:T(8,128)}) fusion(f32[512,256,6]{1,0,2:T(8,128)S(1)} %fusion.9), kind=kOutput, calls=%fused_computation.64 | output fusion | flops 1573375 | bytes 6297600 | tf_op jit(solution)/shard_map/sub | solution.py:154
  130.2 7.3 %convolution_convert_fusion = bf16[6,512,1024]{2,1,0:T(8,128)(2,1)} fusion(bf16[256,6,1024]{2,0,1:T(8,128)(2,1)S(1)} %copy-done, f32[256,6]{0,1:T(8,128)S(1)} %get-tuple-element.123, f32[512,256,6]{1,0,2:T(8,128)} %copy-done.3), kind=kOutput, calls=%fused_computation.1 | convolution fusion | flops 1616119808 | bytes 12589056 | tf_op jit(solution)/shard_map/tbs,tbd->bsd/dot_general | solution.py:155
  137.5 5.7 %fusion.1 = (f32[256,6]{0,1:T(8,128)S(1)}, f32[6,512,256]{2,1,0:T(8,128)S(1)}) fusion(f32[256,6,512]{0,2,1:T(8,128)} %get-tuple-element.124, f32[256,6]{0,1:T(8,128)S(1)} %get-tuple-element.123, bf16[6,512,1024]{2,1,0:T(8,128)(2,1)} %copy-done.21, bf16[256,6,1024]{2,0,1:T(8,128)(2,1)S(1)} %copy-done), kind=kOutput, calls=%fused_computation.4 | convolution fusion | flops 1612970496 | bytes 15740928 | tf_op jit(solution)/shard_map/tbd,bsd->tbs/dot_general | solution.py:162
  145.2 1.8 fusion.27
  147.3 3.4 %collective-permute-start.39 = (bf16[512,256]{1,0:T(8,128)(2,1)S(1)}, bf16[512,256]{1,0:T(8,128)(2,1)S(1)}, u32[]{:S(2)}, u32[]{:S(2)}) collective-permute-start(bf16[512,256]{1,0:T(8,128)(2,1)S(1)} %get-tuple-element.111), channel_id=1, source_target_pairs={{0,16},{8,24},{16,0},{24,8},{1,17},{9,25},{17,1},{25,9},{2,18},{10... | collective-permute-start | bytes 786440 | tf_op jit(solution)/shard_map/ppermute | solution.py:20
  154.5 6.3 %collective-permute-done.38 = bf16[512,256]{1,0:T(8,128)(2,1)S(1)} collective-permute-done((bf16[512,256]{1,0:T(8,128)(2,1)S(1)}, bf16[512,256]{1,0:T(8,128)(2,1)S(1)}, u32[]{:S(2)}, u32[]{:S(2)}) %collective-permute-start.38) | collective-permute-done | bytes 262176 | tf_op jit(solution)/shard_map/ppermute | solution.py:20
  160.9 8.2 %collective-permute-done.39 = bf16[512,256]{1,0:T(8,128)(2,1)S(1)} collective-permute-done((bf16[512,256]{1,0:T(8,128)(2,1)S(1)}, bf16[512,256]{1,0:T(8,128)(2,1)S(1)}, u32[]{:S(2)}, u32[]{:S(2)}) %collective-permute-start.39) | collective-permute-done | bytes 262176 | tf_op jit(solution)/shard_map/ppermute | solution.py:20
  171.5 3.7 %collective-permute-done.25.refs_2_ = bf16[6,16,1024]{2,1,0:T(8,128)(2,1)S(1)} collective-permute-done((bf16[6,16,1024]{2,1,0:T(8,128)(2,1)S(1)}, bf16[6,16,1024]{2,1,0:T(8,128)(2,1)S(1)}, u32[]{:S(2)}, u32[]{:S(2)}) %collective-permute-start.25) | collective-permute-done | bytes 196640 | tf_op jit(solution)/shard_map/ppermute | solution.py:20
  179.7 2.3 collective-permute-start.33
  185.8 1.9 collective-permute-start.37
  187.8 3.5 %convolution_convert_fusion.1 = bf16[256,6,1024]{2,0,1:T(8,128)(2,1)} fusion(bf16[256,6,512]{0,2,1:T(8,128)(2,1)S(1)} %fusion.3, bf16[512,256]{1,0:T(8,128)(2,1)S(1)} %copy-done.12, bf16[512,256]{1,0:T(8,128)(2,1)S(1)} %copy-done.14, bf16[512,256]{1,0:T(8,128)(2,1)S(1)} %copy-done.16, bf16[512,256]{1,0:T(8,128)(2,1)S(1)} %get-tuple-element.112), kind=kOutput, calls=%fused_computation.11 | convolution fusion | flops 1616379904 | bytes 5767168 | tf_op jit(solution)/shard_map/tbs,sd->tbd/dot_general | solution.py:167
  191.3 4.5 %collective-permute-done.33.refs_3_ = bf16[6,48,1024]{2,1,0:T(8,128)(2,1)S(1)} collective-permute-done((bf16[6,48,1024]{2,1,0:T(8,128)(2,1)S(1)}, bf16[6,48,1024]{2,1,0:T(8,128)(2,1)S(1)}, u32[]{:S(2)}, u32[]{:S(2)}) %collective-permute-start.33) | collective-permute-done | bytes 589856 | tf_op jit(solution)/shard_map/ppermute | solution.py:20
  195.8 2.1 collective-permute-start.26
  197.9 26.9 %collective-permute-done.34.refs_4_ = bf16[6,48,1024]{2,1,0:T(8,128)(2,1)S(1)} collective-permute-done((bf16[6,48,1024]{2,1,0:T(8,128)(2,1)S(1)}, bf16[6,48,1024]{2,1,0:T(8,128)(2,1)S(1)}, u32[]{:S(2)}, u32[]{:S(2)}) %collective-permute-start.34) | collective-permute-done | bytes 589856 | tf_op jit(solution)/shard_map/ppermute | solution.py:20
  225.3 10.2 %collective-permute-done.35.refs_5_ = bf16[6,48,1024]{2,1,0:T(8,128)(2,1)S(1)} collective-permute-done((bf16[6,48,1024]{2,1,0:T(8,128)(2,1)S(1)}, bf16[6,48,1024]{2,1,0:T(8,128)(2,1)S(1)}, u32[]{:S(2)}, u32[]{:S(2)}) %collective-permute-start.35) | collective-permute-done | bytes 589856 | tf_op jit(solution)/shard_map/ppermute | solution.py:20
  235.5 1.9 collective-permute-start.28
  237.4 1.8 collective-permute-start.29
  240.0 9.4 %shard_map.69.refs_8_ = bf16[64,48,1024]{2,1,0:T(8,128)(2,1)} custom-call(s32[1]{0:T(128)} %bitcast.10.me_ref, bf16[6,48,1024]{2,1,0:T(8,128)(2,1)} %get-tuple-element.100.refs_0_, bf16[6,48,1024]{2,1,0:T(8,128)(2,1)} %copy-done.4, bf16[6,48,1024]{2,1,0:T(8,128)(2,1)} %collective-permute-done.32.refs_2_, bf16[6,48,1024]{2,1,0:T(8,128)(2,1)} %copy-done.5, ...), custom_call_target="tpu_custom_call" | custom-call | tf_op jit(solution)/shard_map/pallas_call | solution.py:85
  250.9 4.1 %shard_map.70 = bf16[64,48,1024]{2,1,0:T(8,128)(2,1)} custom-call(s32[1]{0:T(128)} %bitcast.10.me_ref, bf16[6,16,1024]{2,1,0:T(8,128)(2,1)} %get-tuple-element.108.refs_0_, bf16[6,16,1024]{2,1,0:T(8,128)(2,1)} %copy-done.17, bf16[6,16,1024]{2,1,0:T(8,128)(2,1)} %copy-done.18, bf16[6,16,1024]{2,1,0:T(8,128)(2,1)} %copy-done.19, ...), custom_call_target="tpu_custom_call", output_to_operand_aliasing={{}: (9, {})} | custom-call | tf_op jit(solution)/shard_map/pallas_call | solution.py:85
  (161 shorter events, 58.0 us)
Async XLA Ops:
  4.7 12.1 %collective-permute-start.3 = (bf16[64,256]{1,0:T(8,128)(2,1)S(1)}, bf16[64,256]{1,0:T(8,128)(2,1)S(1)}, u32[]{:S(2)}, u32[]{:S(2)}) collective-permute-start(bf16[64,256]{1,0:T(8,128)(2,1)S(1)} %constant_dynamic-slice_fusion.3), channel_id=1, source_target_pairs={{0,4},{1,5},{2,6},{3,7},{4,0},{5,1},{6,2},{7,3},{8,12},{9,13},{10,... | collective-permute-start | bytes 98312 | tf_op jit(solution)/shard_map/ppermute | solution.py:20
  6.4 11.7 %collective-permute-start.5 = (bf16[64,256]{1,0:T(8,128)(2,1)S(1)}, bf16[64,256]{1,0:T(8,128)(2,1)S(1)}, u32[]{:S(2)}, u32[]{:S(2)}) collective-permute-start(bf16[64,256]{1,0:T(8,128)(2,1)S(1)} %constant_dynamic-slice_fusion.3), channel_id=1, source_target_pairs={{0,6},{1,7},{2,4},{3,5},{4,2},{5,3},{6,0},{7,1},{8,14},{9,15},{10,... | collective-permute-start | bytes 98312 | tf_op jit(solution)/shard_map/ppermute | solution.py:20
  16.0 23.8 %collective-permute-start.10 = (bf16[6,32,1024]{2,1,0:T(8,128)(2,1)}, bf16[6,32,1024]{2,1,0:T(8,128)(2,1)}, u32[]{:S(2)}, u32[]{:S(2)}) collective-permute-start(bf16[6,32,1024]{2,1,0:T(8,128)(2,1)} %get-tuple-element.60), channel_id=1, source_target_pairs={{0,1},{1,0},{2,3},{3,2},{4,5},{5,4},{6,7},{7,6},{8,9},{9,8},{10,11... | collective-permute-start | bytes 1179656 | tf_op jit(solution)/shard_map/ppermute | solution.py:20
  16.7 25.0 %collective-permute-start.11 = (bf16[6,32,1024]{2,1,0:T(8,128)(2,1)}, bf16[6,32,1024]{2,1,0:T(8,128)(2,1)}, u32[]{:S(2)}, u32[]{:S(2)}) collective-permute-start(bf16[6,32,1024]{2,1,0:T(8,128)(2,1)} %get-tuple-element.61), channel_id=1, source_target_pairs={{0,2},{1,3},{2,0},{3,1},{4,6},{5,7},{6,4},{7,5},{8,10},{9,11},{10,... | collective-permute-start | bytes 1179656 | tf_op jit(solution)/shard_map/ppermute | solution.py:20
  18.0 24.9 %collective-permute-start.12 = (bf16[6,32,1024]{2,1,0:T(8,128)(2,1)}, bf16[6,32,1024]{2,1,0:T(8,128)(2,1)}, u32[]{:S(2)}, u32[]{:S(2)}) collective-permute-start(bf16[6,32,1024]{2,1,0:T(8,128)(2,1)} %get-tuple-element.62), channel_id=1, source_target_pairs={{0,3},{1,2},{2,1},{3,0},{4,7},{5,6},{6,5},{7,4},{8,11},{9,10},{10,... | collective-permute-start | bytes 1179656 | tf_op jit(solution)/shard_map/ppermute | solution.py:20
  18.2 24.7 %collective-permute-start.13 = (bf16[6,32,1024]{2,1,0:T(8,128)(2,1)}, bf16[6,32,1024]{2,1,0:T(8,128)(2,1)}, u32[]{:S(2)}, u32[]{:S(2)}) collective-permute-start(bf16[6,32,1024]{2,1,0:T(8,128)(2,1)} %get-tuple-element.63), channel_id=1, source_target_pairs={{0,4},{1,5},{2,6},{3,7},{4,0},{5,1},{6,2},{7,3},{8,12},{9,13},{10,... | collective-permute-start | bytes 1179656 | tf_op jit(solution)/shard_map/ppermute | solution.py:20
  24.4 15.3 %collective-permute-start.8 = (bf16[512,256]{1,0:T(8,128)(2,1)}, bf16[512,256]{1,0:T(8,128)(2,1)}, u32[]{:S(2)}, u32[]{:S(2)}) collective-permute-start(bf16[512,256]{1,0:T(8,128)(2,1)} %constant_dynamic-update-slice_fusion), channel_id=1, source_target_pairs={{0,16},{8,24},{16,0},{24,8},{1,17},{9,25},{17,1},{25,9},{2,18},{10... | collective-permute-start | bytes 786440 | tf_op jit(solution)/shard_map/ppermute | solution.py:20
  39.7 28.2 %collective-permute-start.14 = (bf16[6,32,1024]{2,1,0:T(8,128)(2,1)}, bf16[6,32,1024]{2,1,0:T(8,128)(2,1)}, u32[]{:S(2)}, u32[]{:S(2)}) collective-permute-start(bf16[6,32,1024]{2,1,0:T(8,128)(2,1)} %get-tuple-element.64), channel_id=1, source_target_pairs={{0,5},{1,4},{2,7},{3,6},{4,1},{5,0},{6,3},{7,2},{8,13},{9,12},{10,... | collective-permute-start | bytes 1179656 | tf_op jit(solution)/shard_map/ppermute | solution.py:20
  39.8 29.0 %collective-permute-start.15 = (bf16[6,32,1024]{2,1,0:T(8,128)(2,1)}, bf16[6,32,1024]{2,1,0:T(8,128)(2,1)}, u32[]{:S(2)}, u32[]{:S(2)}) collective-permute-start(bf16[6,32,1024]{2,1,0:T(8,128)(2,1)} %get-tuple-element.65), channel_id=1, source_target_pairs={{0,6},{1,7},{2,4},{3,5},{4,2},{5,3},{6,0},{7,1},{8,14},{9,15},{10,... | collective-permute-start | bytes 1179656 | tf_op jit(solution)/shard_map/ppermute | solution.py:20
  41.8 28.3 %collective-permute-start.16 = (bf16[6,32,1024]{2,1,0:T(8,128)(2,1)}, bf16[6,32,1024]{2,1,0:T(8,128)(2,1)}, u32[]{:S(2)}, u32[]{:S(2)}) collective-permute-start(bf16[6,32,1024]{2,1,0:T(8,128)(2,1)} %get-tuple-element.66), channel_id=1, source_target_pairs={{0,7},{1,6},{2,5},{3,4},{4,3},{5,2},{6,1},{7,0},{8,15},{9,14},{10,... | collective-permute-start | bytes 1179656 | tf_op jit(solution)/shard_map/ppermute | solution.py:20
  42.9 28.1 %collective-permute-start.17 = (bf16[6,32,1024]{2,1,0:T(8,128)(2,1)}, bf16[6,32,1024]{2,1,0:T(8,128)(2,1)}, u32[]{:S(2)}, u32[]{:S(2)}) collective-permute-start(bf16[6,32,1024]{2,1,0:T(8,128)(2,1)} %get-tuple-element.68), channel_id=1, source_target_pairs={{0,1},{1,0},{2,3},{3,2},{4,5},{5,4},{6,7},{7,6},{8,9},{9,8},{10,11... | collective-permute-start | bytes 1179656 | tf_op jit(solution)/shard_map/ppermute | solution.py:20
  42.9 29.0 %collective-permute-start.18 = (bf16[6,32,1024]{2,1,0:T(8,128)(2,1)}, bf16[6,32,1024]{2,1,0:T(8,128)(2,1)}, u32[]{:S(2)}, u32[]{:S(2)}) collective-permute-start(bf16[6,32,1024]{2,1,0:T(8,128)(2,1)} %get-tuple-element.69), channel_id=1, source_target_pairs={{0,2},{1,3},{2,0},{3,1},{4,6},{5,7},{6,4},{7,5},{8,10},{9,11},{10,... | collective-permute-start | bytes 1179656 | tf_op jit(solution)/shard_map/ppermute | solution.py:20
  68.8 29.2 %collective-permute-start.20 = (bf16[6,32,1024]{2,1,0:T(8,128)(2,1)}, bf16[6,32,1024]{2,1,0:T(8,128)(2,1)}, u32[]{:S(2)}, u32[]{:S(2)}) collective-permute-start(bf16[6,32,1024]{2,1,0:T(8,128)(2,1)} %get-tuple-element.71), channel_id=1, source_target_pairs={{0,4},{1,5},{2,6},{3,7},{4,0},{5,1},{6,2},{7,3},{8,12},{9,13},{10,... | collective-permute-start | bytes 1179656 | tf_op jit(solution)/shard_map/ppermute | solution.py:20
  70.1 35.9 %collective-permute-start.21 = (bf16[6,32,1024]{2,1,0:T(8,128)(2,1)}, bf16[6,32,1024]{2,1,0:T(8,128)(2,1)}, u32[]{:S(2)}, u32[]{:S(2)}) collective-permute-start(bf16[6,32,1024]{2,1,0:T(8,128)(2,1)} %get-tuple-element.72), channel_id=1, source_target_pairs={{0,5},{1,4},{2,7},{3,6},{4,1},{5,0},{6,3},{7,2},{8,13},{9,12},{10,... | collective-permute-start | bytes 1179656 | tf_op jit(solution)/shard_map/ppermute | solution.py:20
  70.9 35.1 %collective-permute-start.22 = (bf16[6,32,1024]{2,1,0:T(8,128)(2,1)}, bf16[6,32,1024]{2,1,0:T(8,128)(2,1)}, u32[]{:S(2)}, u32[]{:S(2)}) collective-permute-start(bf16[6,32,1024]{2,1,0:T(8,128)(2,1)} %get-tuple-element.73), channel_id=1, source_target_pairs={{0,6},{1,7},{2,4},{3,5},{4,2},{5,3},{6,0},{7,1},{8,14},{9,15},{10,... | collective-permute-start | bytes 1179656 | tf_op jit(solution)/shard_map/ppermute | solution.py:20
  71.9 34.2 %collective-permute-start.23 = (bf16[6,32,1024]{2,1,0:T(8,128)(2,1)}, bf16[6,32,1024]{2,1,0:T(8,128)(2,1)}, u32[]{:S(2)}, u32[]{:S(2)}) collective-permute-start(bf16[6,32,1024]{2,1,0:T(8,128)(2,1)} %get-tuple-element.74), channel_id=1, source_target_pairs={{0,7},{1,6},{2,5},{3,4},{4,3},{5,2},{6,1},{7,0},{8,15},{9,14},{10,... | collective-permute-start | bytes 1179656 | tf_op jit(solution)/shard_map/ppermute | solution.py:20
  79.6 42.0 %collective-permute-start.7 = (bf16[512,256]{1,0:T(8,128)(2,1)}, bf16[512,256]{1,0:T(8,128)(2,1)S(1)}, u32[]{:S(2)}, u32[]{:S(2)}) collective-permute-start(bf16[512,256]{1,0:T(8,128)(2,1)} %constant_dynamic-update-slice_fusion), channel_id=1, source_target_pairs={{0,8},{8,0},{16,24},{24,16},{1,9},{9,1},{17,25},{25,17},{2,10},{10... | collective-permute-start | bytes 786440 | tf_op jit(solution)/shard_map/ppermute | solution.py:20
  98.0 23.7 %collective-permute-start.9 = (bf16[512,256]{1,0:T(8,128)(2,1)}, bf16[512,256]{1,0:T(8,128)(2,1)S(1)}, u32[]{:S(2)}, u32[]{:S(2)}) collective-permute-start(bf16[512,256]{1,0:T(8,128)(2,1)} %collective-permute-done.8), channel_id=1, source_target_pairs={{0,8},{8,0},{16,24},{24,16},{1,9},{9,1},{17,25},{25,17},{2,10},{10... | collective-permute-start | bytes 786440 | tf_op jit(solution)/shard_map/ppermute | solution.py:20
  147.1 13.8 %collective-permute-start.38 = (bf16[512,256]{1,0:T(8,128)(2,1)S(1)}, bf16[512,256]{1,0:T(8,128)(2,1)S(1)}, u32[]{:S(2)}, u32[]{:S(2)}) collective-permute-start(bf16[512,256]{1,0:T(8,128)(2,1)S(1)} %get-tuple-element.109), channel_id=1, source_target_pairs={{0,8},{8,0},{16,24},{24,16},{1,9},{9,1},{17,25},{25,17},{2,10},{10... | collective-permute-start | bytes 786440 | tf_op jit(solution)/shard_map/ppermute | solution.py:20
  147.3 21.8 %collective-permute-start.39 = (bf16[512,256]{1,0:T(8,128)(2,1)S(1)}, bf16[512,256]{1,0:T(8,128)(2,1)S(1)}, u32[]{:S(2)}, u32[]{:S(2)}) collective-permute-start(bf16[512,256]{1,0:T(8,128)(2,1)S(1)} %get-tuple-element.111), channel_id=1, source_target_pairs={{0,16},{8,24},{16,0},{24,8},{1,17},{9,25},{17,1},{25,9},{2,18},{10... | collective-permute-start | bytes 786440 | tf_op jit(solution)/shard_map/ppermute | solution.py:20
  150.7 19.0 %collective-permute-start.40 = (bf16[512,256]{1,0:T(8,128)(2,1)S(1)}, bf16[512,256]{1,0:T(8,128)(2,1)S(1)}, u32[]{:S(2)}, u32[]{:S(2)}) collective-permute-start(bf16[512,256]{1,0:T(8,128)(2,1)S(1)} %get-tuple-element.110), channel_id=1, source_target_pairs={{0,24},{8,16},{16,8},{24,0},{1,25},{9,17},{17,9},{25,1},{2,26},{10... | collective-permute-start | bytes 786440 | tf_op jit(solution)/shard_map/ppermute | solution.py:20
  153.1 31.9 %collective-permute-start.31 = (bf16[6,48,1024]{2,1,0:T(8,128)(2,1)S(1)}, bf16[6,48,1024]{2,1,0:T(8,128)(2,1)S(1)}, u32[]{:S(2)}, u32[]{:S(2)}) collective-permute-start(bf16[6,48,1024]{2,1,0:T(8,128)(2,1)S(1)} %get-tuple-element.99), channel_id=1, source_target_pairs={{0,1},{1,0},{2,3},{3,2},{4,5},{5,4},{6,7},{7,6},{8,9},{9,8},{10,11... | collective-permute-start | bytes 1769480 | tf_op jit(solution)/shard_map/ppermute | solution.py:20
  153.1 32.7 %collective-permute-start.32 = (bf16[6,48,1024]{2,1,0:T(8,128)(2,1)S(1)}, bf16[6,48,1024]{2,1,0:T(8,128)(2,1)}, u32[]{:S(2)}, u32[]{:S(2)}) collective-permute-start(bf16[6,48,1024]{2,1,0:T(8,128)(2,1)S(1)} %get-tuple-element.98), channel_id=1, source_target_pairs={{0,2},{1,3},{2,0},{3,1},{4,6},{5,7},{6,4},{7,5},{8,10},{9,11},{10,... | collective-permute-start | bytes 1769480 | tf_op jit(solution)/shard_map/ppermute | solution.py:20
  179.7 16.1 %collective-permute-start.33 = (bf16[6,48,1024]{2,1,0:T(8,128)(2,1)S(1)}, bf16[6,48,1024]{2,1,0:T(8,128)(2,1)S(1)}, u32[]{:S(2)}, u32[]{:S(2)}) collective-permute-start(bf16[6,48,1024]{2,1,0:T(8,128)(2,1)S(1)} %get-tuple-element.97), channel_id=1, source_target_pairs={{0,3},{1,2},{2,1},{3,0},{4,7},{5,6},{6,5},{7,4},{8,11},{9,10},{10,... | collective-permute-start | bytes 1769480 | tf_op jit(solution)/shard_map/ppermute | solution.py:20
  183.3 41.5 %collective-permute-start.34 = (bf16[6,48,1024]{2,1,0:T(8,128)(2,1)S(1)}, bf16[6,48,1024]{2,1,0:T(8,128)(2,1)S(1)}, u32[]{:S(2)}, u32[]{:S(2)}) collective-permute-start(bf16[6,48,1024]{2,1,0:T(8,128)(2,1)S(1)} %get-tuple-element.96), channel_id=1, source_target_pairs={{0,4},{1,5},{2,6},{3,7},{4,0},{5,1},{6,2},{7,3},{8,12},{9,13},{10,... | collective-permute-start | bytes 1769480 | tf_op jit(solution)/shard_map/ppermute | solution.py:20
  184.0 51.5 %collective-permute-start.35 = (bf16[6,48,1024]{2,1,0:T(8,128)(2,1)S(1)}, bf16[6,48,1024]{2,1,0:T(8,128)(2,1)S(1)}, u32[]{:S(2)}, u32[]{:S(2)}) collective-permute-start(bf16[6,48,1024]{2,1,0:T(8,128)(2,1)S(1)} %get-tuple-element.95), channel_id=1, source_target_pairs={{0,5},{1,4},{2,7},{3,6},{4,1},{5,0},{6,3},{7,2},{8,13},{9,12},{10,... | collective-permute-start | bytes 1769480 | tf_op jit(solution)/shard_map/ppermute | solution.py:20
  185.1 52.3 %collective-permute-start.36 = (bf16[6,48,1024]{2,1,0:T(8,128)(2,1)S(1)}, bf16[6,48,1024]{2,1,0:T(8,128)(2,1)S(1)}, u32[]{:S(2)}, u32[]{:S(2)}) collective-permute-start(bf16[6,48,1024]{2,1,0:T(8,128)(2,1)S(1)} %get-tuple-element.94), channel_id=1, source_target_pairs={{0,6},{1,7},{2,4},{3,5},{4,2},{5,3},{6,0},{7,1},{8,14},{9,15},{10,... | collective-permute-start | bytes 1769480 | tf_op jit(solution)/shard_map/ppermute | solution.py:20
  185.8 53.3 %collective-permute-start.37 = (bf16[6,48,1024]{2,1,0:T(8,128)(2,1)S(1)}, bf16[6,48,1024]{2,1,0:T(8,128)(2,1)S(1)}, u32[]{:S(2)}, u32[]{:S(2)}) collective-permute-start(bf16[6,48,1024]{2,1,0:T(8,128)(2,1)S(1)} %get-tuple-element.93), channel_id=1, source_target_pairs={{0,7},{1,6},{2,5},{3,4},{4,3},{5,2},{6,1},{7,0},{8,15},{9,14},{10,... | collective-permute-start | bytes 1769480 | tf_op jit(solution)/shard_map/ppermute | solution.py:20
  195.8 53.6 %collective-permute-start.26 = (bf16[6,16,1024]{2,1,0:T(8,128)(2,1)}, bf16[6,16,1024]{2,1,0:T(8,128)(2,1)S(1)}, u32[]{:S(2)}, u32[]{:S(2)}) collective-permute-start(bf16[6,16,1024]{2,1,0:T(8,128)(2,1)} %get-tuple-element.105), channel_id=1, source_target_pairs={{0,3},{1,2},{2,1},{3,0},{4,7},{5,6},{6,5},{7,4},{8,11},{9,10},{10,... | collective-permute-start | bytes 589832 | tf_op jit(solution)/shard_map/ppermute | solution.py:20
  224.8 24.7 %collective-permute-start.27 = (bf16[6,16,1024]{2,1,0:T(8,128)(2,1)}, bf16[6,16,1024]{2,1,0:T(8,128)(2,1)S(1)}, u32[]{:S(2)}, u32[]{:S(2)}) collective-permute-start(bf16[6,16,1024]{2,1,0:T(8,128)(2,1)} %get-tuple-element.104), channel_id=1, source_target_pairs={{0,4},{1,5},{2,6},{3,7},{4,0},{5,1},{6,2},{7,3},{8,12},{9,13},{10,... | collective-permute-start | bytes 589832 | tf_op jit(solution)/shard_map/ppermute | solution.py:20
  235.5 15.4 %collective-permute-start.28 = (bf16[6,16,1024]{2,1,0:T(8,128)(2,1)}, bf16[6,16,1024]{2,1,0:T(8,128)(2,1)}, u32[]{:S(2)}, u32[]{:S(2)}) collective-permute-start(bf16[6,16,1024]{2,1,0:T(8,128)(2,1)} %get-tuple-element.103), channel_id=1, source_target_pairs={{0,5},{1,4},{2,7},{3,6},{4,1},{5,0},{6,3},{7,2},{8,13},{9,12},{10,... | collective-permute-start | bytes 589832 | tf_op jit(solution)/shard_map/ppermute | solution.py:20
  237.4 13.5 %collective-permute-start.29 = (bf16[6,16,1024]{2,1,0:T(8,128)(2,1)}, bf16[6,16,1024]{2,1,0:T(8,128)(2,1)}, u32[]{:S(2)}, u32[]{:S(2)}) collective-permute-start(bf16[6,16,1024]{2,1,0:T(8,128)(2,1)} %get-tuple-element.102), channel_id=1, source_target_pairs={{0,6},{1,7},{2,4},{3,5},{4,2},{5,3},{6,0},{7,1},{8,14},{9,15},{10,... | collective-permute-start | bytes 589832 | tf_op jit(solution)/shard_map/ppermute | solution.py:20
  (42 other events, 570.1 us)
